TPU v7x, 256 devices: a 2x2x32 block of a 4x8x32 slice. The times are simulated.
256 devices in a mesh: real: 4 (over y, x), row: 64 (over z, core).
Axes of the slice: x: 2, y: 2, z: 32, core: 2. Of those that a mesh axis runs over, the one named last changes fastest.
The devices are a block of a 4x8x32 slice.
Arguments:
- site_tensor: float32 [256, 2, 256, 256], P(('real', 'row')), parts along dimension 0, may hold values from -20 to 20
- left_env: float32 [256, 14, 256, 256], P(('real', 'row')), parts along dimension 0, may hold values from -10 to 10
- right_env: float32 [256, 14, 256, 256], P(('real', 'row')), parts along dimension 0, may hold values from -10 to 10
- sector_size: int32 [256], P('real'), parts along dimension 0, may hold values from 64 to 256
Outputs:
- left_out: float32 [256, 2, 256, 256], P(('real', 'row')), parts along dimension 0
- bond_out: float32 [256, 256, 256], P(('real', 'row')), parts along dimension 0
There are 4 independent parts, one for each index of `real`. A program takes and returns all parts, laid end to end along the dimension named above; each array names one. Nothing has to cross between parts.
All inputs are finite; a program needn't handle non-finite values.
Results may differ from a plain program's by a relative error of at most 0.00005.
Values sent between devices are 32-bit elements; how exact they have to be, the bound alone decides.
A program may use at most 64 MiB of HBM per device.

v0:
```python
import functools

import jax
import jax.numpy as jnp
from jax import lax
from jax.experimental import pallas as pl
from jax.experimental.pallas import tpu as pltpu
from jax.sharding import PartitionSpec as P

MESH = pl.DeviceIdType.MESH
W_DN = 4
W_UP = 4
HALO = W_DN + W_UP
TAU = 0.15
BLK = 64
highest = lax.Precision.HIGHEST
f32 = jnp.float32
bf16 = jnp.bfloat16


def across_lanes(tile, lane):
    return jnp.broadcast_to(tile[:, lane : lane + 1], tile.shape)


def across_rows(tile, row):
    return jnp.broadcast_to(tile[row : row + 1, :], tile.shape)


def eliminate(tiles, first):
    sub = lax.broadcasted_iota(jnp.int32, (8, 128), 0)
    count = len(tiles)
    tiles = list(tiles)
    for g in range(count):
        cols = {v: [across_lanes(tiles[v], first + 8 * g + j) for j in range(8)] for v in range(g, count)}
        pivots = None
        for j in range(8):
            pivot = across_rows(cols[g][j], j)
            inverse = 1.0 / pivot
            pivots = pivot if pivots is None else jnp.where(sub == j, pivot, pivots)
            row = across_rows(tiles[g], j) * inverse
            heads = [across_rows(cols[g][k], j) * inverse for k in range(j + 1, 8)]
            below = jnp.where(sub > j, cols[g][j], 0.0)
            for v in range(g, count):
                factor = below if v == g else cols[v][j]
                for k in range(j + 1, 8):
                    cols[v][k] = cols[v][k] - factor * heads[k - j - 1]
                tiles[v] = tiles[v] - factor * row
        tiles[g] = tiles[g] * lax.rsqrt(pivots)
    return tiles


def dot(a, b, dims=((1,), (0,)), precision=None):
    return lax.dot_general(a, b, (dims, ((), ())), precision=precision, preferred_element_type=f32)


def split(x):
    high = x.astype(bf16)
    return high, (x - high.astype(f32)).astype(bf16)


def dot3(ah, al, bh, bl):
    return dot(ah, bh) + dot(ah, bl) + dot(al, bh)


def factorize(gram, upper, bond, diag_inverse, mask_pair, done):
    size = gram.shape[0]
    for k in range(size // BLK):
        r0 = k * BLK
        c0 = r0 // 128 * 128
        first = r0 - c0
        lane = lax.broadcasted_iota(jnp.int32, (8, 128), 1)
        sub = lax.broadcasted_iota(jnp.int32, (8, 128), 0)
        in_block = (lane >= first) & (lane < first + BLK)
        other = BLK - first
        tiles = []
        for g in range(BLK // 8):
            unit = (lane - other == sub + 8 * g).astype(f32)
            tiles.append(jnp.where(in_block, gram[r0 + 8 * g : r0 + 8 * g + 8, c0 : c0 + 128], unit))
        tiles = eliminate(tiles, first)
        both = jnp.concatenate(tiles, axis=0)
        lane_b = lax.broadcasted_iota(jnp.int32, (BLK, 128), 1)
        row_b = lax.broadcasted_iota(jnp.int32, (BLK, 128), 0)
        in_b = (lane_b >= first) & (lane_b < first + BLK)
        inverse = jnp.where(in_b, 0.0, both)
        diag_inverse[k] = inverse
        rows = gram[r0 : r0 + BLK, c0:]
        panel = dot(inverse, jnp.concatenate([rows, rows], axis=0), precision=highest)
        head = jnp.where(in_b, both, panel[:, :128])
        head = jnp.where(lane_b - first >= row_b, head, 0.0)
        panel = jnp.concatenate([head, panel[:, 128:]], axis=1) if panel.shape[1] > 128 else head
        upper[r0 : r0 + BLK, c0:] = panel
        bond[r0 : r0 + BLK, c0:] = jnp.where(mask_pair(r0, BLK, c0), panel, 0.0)
        done(k, r0, c0)
        if r0 + BLK < size:
            t0 = (r0 + BLK) // 128 * 128
            tail = panel[:, t0 - c0 :]
            gram[t0:, t0:] = gram[t0:, t0:] - dot(tail, tail, ((0,), (0,)), precision=highest)


def kernel(
    n, sizes, site, left_env, right_env, left_out, bond_out,
    site_v, low_v, left_f, right_f, down_f, up_f, left_h, left_l, right_h, right_l,
    gram, upper, bond, inv, halo_m, halo_p, app, app_m, app_p, second, mix_h, mix_l,
    ortho_v, result_v, mine, slots, partner,
    local_sem, out_sem, site_sem, env_sem, bond_sem, app_sem, low_sem, far_sem, pair_sem, known_sem,
):
    me = lax.axis_index("row")
    size = site.shape[-1]
    width = left_env.shape[1]
    chips = n // 2

    def other(step):
        return {"row": lax.rem(me + step + n, n)}

    after, before = other(1), other(-1)
    pair = {"row": me + 1 - 2 * lax.rem(me, 2)}

    def remote(src, dst, sems, target):
        return pltpu.make_async_remote_copy(
            src_ref=src, dst_ref=dst, send_sem=sems.at[0], recv_sem=sems.at[1], device_id=target, device_id_type=MESH
        )

    load_site = pltpu.make_async_copy(site.at[0], site_v, local_sem.at[0])
    load_left = pltpu.make_async_copy(left_env.at[0], left_f, local_sem.at[1])
    load_right = pltpu.make_async_copy(right_env.at[0, pl.ds(HALO, width - HALO)], right_f, local_sem.at[2])
    load_site.start()
    load_left.start()
    load_right.start()

    barrier = pltpu.get_barrier_semaphore()
    for step in (1, -1, 2, -2):
        pl.semaphore_signal(barrier, inc=1, device_id=other(step), device_id_type=MESH)
    pl.semaphore_wait(barrier, 4)

    move_site = remote(site.at[0, 1], low_v, site_sem, after)
    move_down = remote(right_env.at[0, pl.ds(0, W_DN)], down_f, env_sem.at[0], after)
    move_up = remote(right_env.at[0, pl.ds(W_DN, W_UP)], up_f, env_sem.at[1], before)
    move_site.start()
    move_down.start()
    move_up.start()

    rounds = []
    reach = 1
    while 2 * reach <= chips // 2:
        rounds.append(reach)
        reach *= 2

    def greet(i):
        if i < len(rounds):
            for step in (2 * rounds[i], -2 * rounds[i]):
                pl.semaphore_signal(known_sem.at[i], inc=1, device_id=other(step), device_id_type=MESH)

    def greeted(i):
        if i < len(rounds):
            pl.semaphore_wait(known_sem.at[i], 2)

    greet(0)

    own_size = sizes[me]
    low_size = jnp.where(me == 0, 0, sizes[lax.rem(me + n - 1, n)])

    def mask_pair(r0, rows, c0, row_size=None):
        shape = (rows, size - c0)
        row = lax.broadcasted_iota(jnp.int32, shape, 0) + r0
        lane = lax.broadcasted_iota(jnp.int32, shape, 1) + c0
        return (row < (own_size if row_size is None else row_size)) & (lane < own_size)

    load_site.wait()
    ortho_v[0] = jnp.where(mask_pair(0, size, 0), site_v[0], 0.0)
    gram[...] = dot(ortho_v[0], ortho_v[0], ((0,), (0,)), precision=highest)

    def split_into(source, offset):
        def body(i, _):
            high, low = split(source[i])
            at = pl.ds(pl.multiple_of((i + offset) * size, size), size)
            right_h[at, :] = high
            right_l[at, :] = low
            return 0

        lax.fori_loop(0, source.shape[0], body, 0)

    load_left.wait()

    def split_left(i, _):
        high, low = split(left_f[i])
        left_h[i] = high
        left_l[i] = low
        return 0

    lax.fori_loop(0, width, split_left, 0)
    load_right.wait()
    split_into(right_f, HALO)

    move_site.wait_recv()
    ortho_v[1] = jnp.where(mask_pair(0, size, 0, low_size), low_v[...], 0.0)
    row = lax.broadcasted_iota(jnp.int32, (size, size), 0)
    lane = lax.broadcasted_iota(jnp.int32, (size, size), 1)
    dead = ((row == lane) & (row >= own_size)).astype(f32)
    gram[...] = gram[...] + dot(ortho_v[1], ortho_v[1], ((0,), (0,)), precision=highest) + dead

    sends = []

    def bond_piece(k, r0, c0):
        at = (pl.ds(r0, BLK), pl.ds(c0, size - c0))
        for side, (target, halo) in enumerate(((after, halo_m), (before, halo_p))):
            copy = remote(bond.at[at], halo.at[at], bond_sem.at[side, k], target)
            copy.start()
            sends.append(copy)
        greeted(k)
        greet(k + 1)

    bond[size // 2 :, : size // 2] = jnp.zeros((size // 2, size // 2), f32)
    factorize(gram, upper, bond, inv, mask_pair, bond_piece)
    for i in range(size // BLK, len(rounds)):
        greeted(i)
        greet(i + 1)

    def stage_one(first, last, block):
        high, low = split(block)
        for a in range(first, last):
            mixed = dot3(left_h[a], left_l[a], high, low)
            at = slice(a * size, (a + 1) * size)
            mix_h[:, at], mix_l[:, at] = split(mixed)

    def stage_two(r0, rows):
        at = slice(r0, r0 + rows)
        return dot3(mix_h[at, :], mix_l[at, :], right_h[...], right_l[...])

    stage_one(HALO, width, bond[...])
    move_down.wait_recv()
    split_into(down_f, 0)
    move_up.wait_recv()
    split_into(up_f, W_DN)
    for copy in sends:
        copy.wait_recv()

    half = size // 2

    def bond_halo(ref, valid):
        low = jnp.concatenate([jnp.zeros((half, half), f32), ref[half:, half:]], axis=1)
        return jnp.where(valid, jnp.concatenate([ref[:half, :], low], axis=0), 0.0)

    has_before = jnp.broadcast_to(me, (size, size)) > 0
    has_after = jnp.broadcast_to(me, (size, size)) < n - 1
    stage_one(0, W_DN, bond_halo(halo_m, has_before))
    stage_one(W_DN, HALO, bond_halo(halo_p, has_after))

    app_sends = []
    for part in range(2):
        r0 = part * half
        app[r0 : r0 + half, :] = jnp.where(mask_pair(r0, half, 0), TAU * stage_two(r0, half), 0.0)
        at = pl.ds(r0, half)
        for side, (target, halo) in enumerate(((after, app_m), (before, app_p))):
            copy = remote(app.at[at], halo.at[at], app_sem.at[side, part], target)
            copy.start()
            app_sends.append(copy)

    stage_one(HALO, width, app[...])
    for copy in app_sends:
        copy.wait_recv()
    stage_one(0, W_DN, jnp.where(has_before, app_m[...], 0.0))
    stage_one(W_DN, HALO, jnp.where(has_after, app_p[...], 0.0))
    second[...] = jnp.where(mask_pair(0, size, 0), (0.5 * TAU) * stage_two(0, size), 0.0)

    def total(x):
        return jnp.sum(jnp.sum(x, axis=0, keepdims=True), axis=1, keepdims=True)

    b, a, h = bond[...], app[...], second[...]
    pieces = [total(x) for x in (b * b, b * a, a * a, b * h, a * h, h * h)]
    lane_1 = lax.broadcasted_iota(jnp.int32, (1, 128), 1)
    packed = jnp.zeros((1, 128), f32)
    for i, piece in enumerate(pieces):
        packed = jnp.where(lane_1 == i, piece, packed)
    mine[0] = packed

    def far(d):
        return pltpu.make_async_remote_copy(
            src_ref=mine.at[0], dst_ref=slots.at[d - 1], send_sem=far_sem.at[0, d - 1], recv_sem=far_sem.at[1, d - 1],
            device_id={"row": lax.rem(me + 2 * d, n)}, device_id_type=MESH,
        )

    def send_far(i, _):
        d = chips // 2 + (i + 1) // 2 * (2 * (i % 2) - 1)
        far(d).start()
        return 0

    lax.fori_loop(0, chips - 1, send_far, 0)

    def ortho_rows(part):
        blocks = []
        for k in range(size // BLK):
            r0 = k * BLK
            c0 = r0 // 128 * 128
            want = ortho_v[part][:, c0 : c0 + 128]
            if k:
                done = jnp.concatenate(blocks, axis=1)
                want = want - dot(done, upper[:r0, c0 : c0 + 128], precision=highest)
            first = r0 - c0
            inverse = inv[k][:, BLK - first : 2 * BLK - first]
            blocks.append(dot(want[:, first : first + BLK], inverse, ((1,), (1,)), precision=highest))
        return jnp.concatenate(blocks, axis=1)

    result_v[1] = ortho_rows(1)
    move_low = remote(result_v.at[1], left_out.at[0, 1], low_sem, before)
    move_low.start()
    result_v[0] = ortho_rows(0)
    store_up = pltpu.make_async_copy(result_v.at[0], left_out.at[0, 0], out_sem.at[0])
    store_up.start()

    def take_far(i, _):
        far(i + 1).wait_recv()
        return 0

    lax.fori_loop(0, chips - 1, take_far, 0)
    mine[1] = mine[0] + jnp.sum(slots[...], axis=0)
    swap = remote(mine.at[1], partner, pair_sem, pair)
    swap.start()
    swap.wait_recv()
    sums = mine[1] + partner[...]
    bb, ba, aa, bh, ah, hh = (jnp.broadcast_to(sums[:, i : i + 1], (1, size)) for i in range(6))
    step = ba / bb
    weight_b = 1.0 - step + 0.5 * step * step
    weight_a = 1.0 - step
    norm = (
        weight_b * weight_b * bb + 2.0 * weight_b * weight_a * ba + weight_a * weight_a * aa
        + 2.0 * weight_b * bh + 2.0 * weight_a * ah + hh
    )
    scale = jnp.sqrt(bb / norm)
    bond_out[0] = (weight_b * bond[...] + weight_a * app[...] + second[...]) * scale

    def sent_far(i, _):
        far(i + 1).wait_send()
        return 0

    lax.fori_loop(0, chips - 1, sent_far, 0)
    for copy in (move_site, move_down, move_up, *sends, *app_sends, swap, move_low):
        copy.wait_send()
    move_low.wait_recv()
    store_up.wait()


def on_device(n, site_tensor, left_env, right_env, sector_size):
    size = site_tensor.shape[-1]
    width = left_env.shape[1]
    full = (size, size)
    hbm = pl.BlockSpec(memory_space=pl.ANY)
    chips = n // 2
    parts = size // BLK
    scratch = [
        pltpu.VMEM((2, *full), f32), pltpu.VMEM(full, f32), pltpu.VMEM((width, *full), f32),
        pltpu.VMEM((width - HALO, *full), f32), pltpu.VMEM((W_DN, *full), f32), pltpu.VMEM((W_UP, *full), f32),
        pltpu.VMEM((width, *full), bf16), pltpu.VMEM((width, *full), bf16),
        pltpu.VMEM((width * size, size), bf16), pltpu.VMEM((width * size, size), bf16),
        pltpu.VMEM(full, f32), pltpu.VMEM(full, f32), pltpu.VMEM(full, f32), pltpu.VMEM((parts, BLK, 128), f32),
        pltpu.VMEM(full, f32), pltpu.VMEM(full, f32), pltpu.VMEM(full, f32), pltpu.VMEM(full, f32),
        pltpu.VMEM(full, f32), pltpu.VMEM(full, f32),
        pltpu.VMEM((size, width * size), bf16), pltpu.VMEM((size, width * size), bf16),
        pltpu.VMEM((2, *full), f32), pltpu.VMEM((2, *full), f32),
        pltpu.VMEM((2, 1, 128), f32), pltpu.VMEM((chips - 1, 1, 128), f32), pltpu.VMEM((1, 128), f32),
        pltpu.SemaphoreType.DMA((3,)), pltpu.SemaphoreType.DMA((1,)), pltpu.SemaphoreType.DMA((2,)),
        pltpu.SemaphoreType.DMA((2, 2)), pltpu.SemaphoreType.DMA((2, parts, 2)), pltpu.SemaphoreType.DMA((2, 2, 2)),
        pltpu.SemaphoreType.DMA((2,)), pltpu.SemaphoreType.DMA((2, chips - 1)), pltpu.SemaphoreType.DMA((2,)),
        pltpu.SemaphoreType.REGULAR((max(1, chips.bit_length()),)),
    ]
    return pl.pallas_call(
        functools.partial(kernel, n),
        out_shape=(
            jax.ShapeDtypeStruct((1, 2, *full), f32),
            jax.ShapeDtypeStruct((1, *full), f32),
        ),
        in_specs=[pl.BlockSpec(memory_space=pltpu.SMEM), hbm, hbm, hbm],
        out_specs=(hbm, pl.BlockSpec(memory_space=pltpu.VMEM)),
        scratch_shapes=scratch,
        compiler_params=pltpu.CompilerParams(
            collective_id=0, has_side_effects=True, vmem_limit_bytes=60 * 1024 * 1024
        ),
    )(sector_size, site_tensor, left_env, right_env)


def solution(mesh):
    block = P(("real", "row"), None, None, None)
    return jax.shard_map(
        functools.partial(on_device, mesh.shape["row"]),
        mesh=mesh,
        in_specs=(block, block, block, P("real")),
        out_specs=(block, P(("real", "row"), None, None)),
        check_vma=False,
    )
```

profile of v0, /device:TPU:37, one launch (start us, length us, event | category | flops | bytes accessed | tf_op | source)
XLA Modules:
  0.0 74.0 jit_solution(5325762453531655168)
XLA Ops:
  0.6 69.8 %shard_map.59 = (f32[1,2,256,256]{3,2,1,0:T(8,128)}, f32[1,256,256]{2,1,0:T(8,128)}) custom-call(s32[64]{0:T(128)} %sizes.1, f32[1,2,256,256]{3,2,1,0:T(8,128)} %site.1, f32[1,14,256,256]{3,2,1,0:T(8,128)} %left_env.1, f32[1,14,256,256]{3,2,1,0:T(8,128)} %right_env.1), custom_call_target="tpu_custom_call" | custom-call | tf_op jit(solution)/shard_map/pallas_call | solution.py:365
  70.4 1.9 %copy.8 = f32[1,2,256,256]{3,2,1,0:T(8,128)} copy(f32[1,2,256,256]{3,2,1,0:T(8,128)} %get-tuple-element.4) | data formatting | bytes 1048576
  72.3 1.7 %copy.9 = f32[1,256,256]{2,1,0:T(8,128)} copy(f32[1,256,256]{2,1,0:T(8,128)} %get-tuple-element.5) | data formatting | bytes 524288
where the time goes:
time: 74.2 us; the launch traced here: 74 us
  Pallas kernels  69.8 us (94%)
  local copies, waits for them, and re-layouts  3.54 us (5%)
    pallas_call x1, Pallas kernels, on_device(): pl.pallas_call(functools.partial(kernel, n), out_shape=(jax.ShapeDtypeStr...  69.8 us
    unnamed x2, local copies, waits for them, and re-layouts  3.54 us

commit v1 on v0

v1 whole, which is shorter than its diff:
```python
import functools

import jax
import jax.numpy as jnp
from jax import lax
from jax.experimental import pallas as pl
from jax.experimental.pallas import tpu as pltpu
from jax.sharding import PartitionSpec as P

MESH = pl.DeviceIdType.MESH
W_DN = 4
W_UP = 4
HALO = W_DN + W_UP
TAU = 0.15
BLK = 64
highest = lax.Precision.HIGHEST
f32 = jnp.float32
bf16 = jnp.bfloat16


def across_lanes(tile, lane):
    return jnp.broadcast_to(tile[:, lane : lane + 1], tile.shape)


def across_rows(tile, row):
    return jnp.broadcast_to(tile[row : row + 1, :], tile.shape)


def eliminate(tiles, first):
    sub = lax.broadcasted_iota(jnp.int32, (8, 128), 0)
    count = len(tiles)
    tiles = [list(tile) for tile in tiles]
    own = [across_lanes(tiles[0][0], first + j) for j in range(8)]
    for g in range(count):
        last = g + 1 == count
        ahead = [] if last else [across_lanes(tiles[g + 1][0], first + 8 * (g + 1) + j) for j in range(8)]
        cols = {v: [across_lanes(tiles[v][0], first + 8 * g + j) for j in range(8)] for v in range(g + 1, count)}
        pivots = None
        for j in range(8):
            pivot = across_rows(own[j], j)
            inverse = 1.0 / pivot
            pivots = pivot if pivots is None else jnp.where(sub == j, pivot, pivots)
            heads = {k: across_rows(own[k], j) * inverse for k in range(j + 1, 8)}
            below = jnp.where(sub > j, own[j], 0.0)
            for k in range(j + 1, 8):
                own[k] = own[k] - below * heads[k]
            rows = [across_rows(part, j) * inverse for part in tiles[g]]
            tiles[g] = [part - below * row for part, row in zip(tiles[g], rows)]
            for v in range(g + 1, count):
                factor = cols[v][j]
                for k in range(j + 1, 8):
                    cols[v][k] = cols[v][k] - factor * heads[k]
                tiles[v] = [part - factor * row for part, row in zip(tiles[v], rows)]
            if not last:
                factor = cols[g + 1][j]
                scaled = factor * inverse
                ahead = [col - factor * across_rows(scaled, k) for k, col in enumerate(ahead)]
        scale = lax.rsqrt(pivots)
        tiles[g] = [part * scale for part in tiles[g]]
        own = ahead
    return tiles


def dot(a, b, dims=((1,), (0,)), precision=None):
    return lax.dot_general(a, b, (dims, ((), ())), precision=precision, preferred_element_type=f32)


def split(x):
    high = x.astype(bf16)
    return high, (x - high.astype(f32)).astype(bf16)


def dot3(ah, al, bh, bl):
    return dot(ah, bh) + dot(ah, bl) + dot(al, bh)


def factorize(gram, upper, bond, diag_inverse, mask_pair, done):
    size = gram.shape[0]
    lane = lax.broadcasted_iota(jnp.int32, (8, 128), 1)
    sub = lax.broadcasted_iota(jnp.int32, (8, 128), 0)
    for k in range(size // BLK):
        r0 = k * BLK
        c0 = r0 // 128 * 128
        first = r0 - c0
        tiles = []
        for g in range(BLK // 8):
            at = slice(r0 + 8 * g, r0 + 8 * g + 8)
            unit = (lane == sub + 8 * g).astype(f32)
            parts = [gram[at, c : c + 128] for c in range(c0, size, 128)]
            if first:
                parts[0] = jnp.where(lane >= first, parts[0], unit)
            else:
                parts.append(unit)
            tiles.append(parts)
        tiles = eliminate(tiles, first)
        parts = [jnp.concatenate([tile[i] for tile in tiles], axis=0) for i in range(len(tiles[0]))]
        diag_inverse[k] = parts[0] if first else parts.pop()
        lane_b = lax.broadcasted_iota(jnp.int32, (BLK, 128), 1)
        row_b = lax.broadcasted_iota(jnp.int32, (BLK, 128), 0)
        parts[0] = jnp.where(lane_b - first >= row_b, parts[0], 0.0)
        panel = jnp.concatenate(parts, axis=1) if len(parts) > 1 else parts[0]
        if r0 + BLK < size:
            if not first:
                turned = jnp.transpose(parts[0])[BLK:, :]
                at = slice(r0 + BLK, r0 + 2 * BLK)
                gram[at, c0:] = gram[at, c0:] - dot(turned, panel, precision=highest)
            if len(parts) > 1:
                turned = jnp.transpose(parts[1])
                gram[c0 + 128 :, c0 + 128 :] = gram[c0 + 128 :, c0 + 128 :] - dot(turned, parts[1], precision=highest)
        upper[r0 : r0 + BLK, c0:] = panel
        bond[r0 : r0 + BLK, c0:] = jnp.where(mask_pair(r0, BLK, c0), panel, 0.0)
        done(k, r0, c0)


def kernel(
    n, sizes, site, left_env, right_env, left_out, bond_out,
    site_v, low_v, left_f, right_f, near_f, cross_f, left_h, left_l, right_h, right_l,
    gram, upper, bond, inv, halo_n, halo_c, app, app_n, app_c, second, part_v, mix_h, mix_l,
    ortho_v, result_v, mine, slots, partner,
    local_sem, out_sem, site_sem, near_sem, cross_sem, bond_sem, app_sem, low_sem, far_sem, pair_sem, known_sem,
):
    me = lax.axis_index("row")
    odd = lax.rem(me, 2)
    size = site.shape[-1]
    half = size // 2
    width = left_env.shape[1]
    own_n = width - HALO
    met_n = own_n + W_DN
    chips = n // 2

    def other(step):
        return {"row": lax.rem(me + step + n, n)}

    near, cross = other(1 - 2 * odd), other(2 * odd - 1)

    def remote(src, dst, sems, target):
        return pltpu.make_async_remote_copy(
            src_ref=src, dst_ref=dst, send_sem=sems.at[0], recv_sem=sems.at[1], device_id=target, device_id_type=MESH
        )

    load_site = pltpu.make_async_copy(site.at[0], site_v, local_sem.at[0])
    load_left = pltpu.make_async_copy(left_env.at[0], left_f, local_sem.at[1])
    load_right = pltpu.make_async_copy(right_env.at[0, pl.ds(HALO, own_n)], right_f, local_sem.at[2])
    load_site.start()
    load_left.start()
    load_right.start()

    barrier = pltpu.get_barrier_semaphore()
    for step in (1, -1, 2, -2):
        pl.semaphore_signal(barrier, inc=1, device_id=other(step), device_id_type=MESH)
    pl.semaphore_wait(barrier, 4)

    def env_piece(i, side):
        at = pl.ds(side * half, half)
        return remote(
            right_env.at[0, W_DN * (1 - odd) + i, :, at], cross_f.at[i, :, at], cross_sem.at[side, i], cross
        )

    load_site.wait()
    move_site = remote(site_v.at[1], low_v, site_sem, other(1))
    move_site.start()
    for i in range(W_DN):
        env_piece(i, 0).start()
    move_near = remote(right_env.at[0, pl.ds(W_DN * odd, W_DN)], near_f, near_sem, near)
    move_near.start()

    rounds = []
    reach = 1
    while 2 * reach <= chips // 2:
        rounds.append(reach)
        reach *= 2

    def greet(i):
        if i < len(rounds):
            for step in (2 * rounds[i], -2 * rounds[i]):
                pl.semaphore_signal(known_sem.at[i], inc=1, device_id=other(step), device_id_type=MESH)

    def greeted(i):
        if i < len(rounds):
            pl.semaphore_wait(known_sem.at[i], 2)

    greet(0)

    own_size = sizes[me]
    low_size = jnp.where(me == 0, 0, sizes[lax.rem(me + n - 1, n)])

    def mask_pair(r0, rows, c0, c1=size, row_size=None):
        shape = (rows, c1 - c0)
        row = lax.broadcasted_iota(jnp.int32, shape, 0) + r0
        lane = lax.broadcasted_iota(jnp.int32, shape, 1) + c0
        return (row < (own_size if row_size is None else row_size)) & (lane < own_size)

    ortho_v[0] = jnp.where(mask_pair(0, size, 0), site_v[0], 0.0)
    row = lax.broadcasted_iota(jnp.int32, (size, size), 0)
    lane = lax.broadcasted_iota(jnp.int32, (size, size), 1)
    dead = ((row == lane) & (row >= own_size)).astype(f32)
    gram[...] = dot(ortho_v[0], ortho_v[0], ((0,), (0,)), precision=highest) + dead

    def split_right(source, offset):
        def body(i, _):
            at = pl.ds(pl.multiple_of((i + offset) * size, size), size)
            right_h[at, :], right_l[at, :] = split(source[i])
            return 0

        lax.fori_loop(0, source.shape[0], body, 0)

    load_left.wait()

    def split_left(count, source, target):
        def body(i, _):
            left_h[i + target], left_l[i + target] = split(left_f[i + source])
            return 0

        lax.fori_loop(0, count, body, 0)

    split_left(own_n, HALO, 0)
    split_left(W_DN, W_DN * (1 - odd), own_n)
    split_left(W_DN, W_DN * odd, met_n)
    load_right.wait()
    split_right(right_f, 0)
    greeted(0)
    greet(1)

    move_site.wait_recv()
    ortho_v[1] = jnp.where(mask_pair(0, size, 0, size, low_size), low_v[...], 0.0)
    gram[...] = gram[...] + dot(ortho_v[1], ortho_v[1], ((0,), (0,)), precision=highest)
    greeted(1)
    greet(2)

    sends = []

    def bond_piece(k, r0, c0):
        at = (pl.ds(r0, BLK), pl.ds(c0, size - c0))
        for side, (target, halo) in enumerate(((near, halo_n), (cross, halo_c))):
            copy = remote(bond.at[at], halo.at[at], bond_sem.at[side, k], target)
            copy.start()
            sends.append(copy)
        if k == 0:
            env_piece(0, 1).start()
            env_piece(1, 1).start()
        if k == size // BLK - 1:
            env_piece(2, 1).start()
            env_piece(3, 1).start()
            greeted(2)
            greet(3)

    bond[half:, :half] = jnp.zeros((half, half), f32)
    factorize(gram, upper, bond, inv, mask_pair, bond_piece)

    def stage_one(first, last, block):
        high, low = split(block)
        for a in range(first, last):
            at = slice(a * size, (a + 1) * size)
            mix_h[:, at], mix_l[:, at] = split(dot3(left_h[a], left_l[a], high, low))

    def stage_two(first, last, c0=0, c1=size):
        at = slice(first * size, last * size)
        return dot3(mix_h[:, at], mix_l[:, at], right_h[at, c0:c1], right_l[at, c0:c1])

    def bond_halo(ref):
        low = jnp.concatenate([jnp.zeros((half, half), f32), ref[half:, half:]], axis=1)
        return jnp.concatenate([ref[:half, :], low], axis=0)

    at_end = jnp.broadcast_to(lax.rem(me + 1, n), (size, size)) < 2
    has_cross = jnp.logical_not(at_end)

    stage_one(0, own_n, bond[...])
    move_near.wait_recv()
    split_right(near_f, own_n)
    for copy in sends[0::2]:
        copy.wait_recv()
    stage_one(own_n, met_n, bond_halo(halo_n))
    part_v[...] = stage_two(0, met_n)

    def ortho_rows(part):
        blocks = []
        for k in range(size // BLK):
            r0 = k * BLK
            c0 = r0 // 128 * 128
            want = ortho_v[part][:, c0 : c0 + 128]
            if k:
                done = jnp.concatenate(blocks, axis=1)
                want = want - dot(done, upper[:r0, c0 : c0 + 128], precision=highest)
            first = r0 - c0
            blocks.append(dot(want[:, first : first + BLK], inv[k][:, :BLK], ((1,), (1,)), precision=highest))
        return jnp.concatenate(blocks, axis=1)

    result_v[1] = ortho_rows(1)
    move_low = remote(result_v.at[1], left_out.at[0, 1], low_sem, other(-1))
    move_low.start()

    for copy in sends[1::2]:
        copy.wait_recv()
    stage_one(met_n, width, jnp.where(has_cross, bond_halo(halo_c), 0.0))

    def split_cross(first, last, side):
        at = slice(side * half, (side + 1) * half)
        for i in range(first, last):
            env_piece(i, side).wait_recv()
            rows = slice((met_n + i) * size, (met_n + i + 1) * size)
            right_h[rows, at], right_l[rows, at] = split(cross_f[i, :, at])

    app_sends = []
    for side in range(2):
        c0, c1 = side * half, (side + 1) * half
        total = part_v[:, c0:c1]
        for i in (0, 2) if side else (0,):
            count = 2 if side else W_DN
            split_cross(i, i + count, side)
            total = total + stage_two(met_n + i, met_n + i + count, c0, c1)
        app[:, c0:c1] = jnp.where(mask_pair(0, size, c0, c1), TAU * total, 0.0)
        at = pl.ds(c0, half)
        for to, (target, halo) in enumerate(((cross, app_c), (near, app_n))):
            copy = remote(app.at[:, at], halo.at[:, at], app_sem.at[to, side], target)
            copy.start()
            app_sends.append(copy)

    def total_of(x):
        return jnp.sum(jnp.sum(x, axis=0, keepdims=True), axis=1, keepdims=True)

    stage_one(0, own_n, app[...])
    for copy in app_sends[1::2]:
        copy.wait_recv()
    stage_one(own_n, met_n, app_n[...])
    part_v[...] = stage_two(0, met_n)
    b, a = bond[...], app[...]
    pieces = [total_of(x) for x in (b * b, b * a, a * a)]
    for copy in app_sends[0::2]:
        copy.wait_recv()
    stage_one(met_n, width, jnp.where(has_cross, app_c[...], 0.0))
    second[...] = jnp.where(mask_pair(0, size, 0), (0.5 * TAU) * (part_v[...] + stage_two(met_n, width)), 0.0)
    h = second[...]
    pieces += [total_of(x) for x in (bond[...] * h, app[...] * h, h * h)]
    lane_1 = lax.broadcasted_iota(jnp.int32, (1, 128), 1)
    packed = jnp.zeros((1, 128), f32)
    for i, piece in enumerate(pieces):
        packed = jnp.where(lane_1 == i, piece, packed)
    mine[0] = packed
    greeted(3)
    for i in range(4, len(rounds)):
        greet(i)
        greeted(i)

    def far(d):
        return pltpu.make_async_remote_copy(
            src_ref=mine.at[0], dst_ref=slots.at[d - 1], send_sem=far_sem.at[0, d - 1], recv_sem=far_sem.at[1, d - 1],
            device_id={"row": lax.rem(me + 2 * d, n)}, device_id_type=MESH,
        )

    def send_far(i, _):
        d = chips // 2 + (i + 1) // 2 * (2 * (i % 2) - 1)
        far(d).start()
        return 0

    lax.fori_loop(0, chips - 1, send_far, 0)

    result_v[0] = ortho_rows(0)
    store_up = pltpu.make_async_copy(result_v.at[0], left_out.at[0, 0], out_sem.at[0])
    store_up.start()

    def take_far(i, _):
        far(i + 1).wait_recv()
        return 0

    lax.fori_loop(0, chips - 1, take_far, 0)
    mine[1] = mine[0] + jnp.sum(slots[...], axis=0)
    swap = remote(mine.at[1], partner, pair_sem, near)
    swap.start()
    swap.wait_recv()
    sums = mine[1] + partner[...]
    bb, ba, aa, bh, ah, hh = (jnp.broadcast_to(sums[:, i : i + 1], (1, size)) for i in range(6))
    step = ba / bb
    weight_b = 1.0 - step + 0.5 * step * step
    weight_a = 1.0 - step
    norm = (
        weight_b * weight_b * bb + 2.0 * weight_b * weight_a * ba + weight_a * weight_a * aa
        + 2.0 * weight_b * bh + 2.0 * weight_a * ah + hh
    )
    scale = jnp.sqrt(bb / norm)
    bond_out[0] = (weight_b * bond[...] + weight_a * app[...] + second[...]) * scale

    def sent_far(i, _):
        far(i + 1).wait_send()
        return 0

    lax.fori_loop(0, chips - 1, sent_far, 0)
    pieces = [env_piece(i, side) for i in range(W_DN) for side in range(2)]
    for copy in (move_site, move_near, *pieces, *sends, *app_sends, swap, move_low):
        copy.wait_send()
    move_low.wait_recv()
    store_up.wait()


def on_device(n, site_tensor, left_env, right_env, sector_size):
    size = site_tensor.shape[-1]
    width = left_env.shape[1]
    full = (size, size)
    hbm = pl.BlockSpec(memory_space=pltpu.HBM)
    chips = n // 2
    parts = size // BLK
    scratch = [
        pltpu.VMEM((2, *full), f32), pltpu.VMEM(full, f32), pltpu.VMEM((width, *full), f32),
        pltpu.VMEM((width - HALO, *full), f32), pltpu.VMEM((W_DN, *full), f32), pltpu.VMEM((W_UP, *full), f32),
        pltpu.VMEM((width, *full), bf16), pltpu.VMEM((width, *full), bf16),
        pltpu.VMEM((width * size, size), bf16), pltpu.VMEM((width * size, size), bf16),
        pltpu.VMEM(full, f32), pltpu.VMEM(full, f32), pltpu.VMEM(full, f32), pltpu.VMEM((parts, BLK, 128), f32),
        *[pltpu.VMEM(full, f32)] * 7,
        pltpu.VMEM((size, width * size), bf16), pltpu.VMEM((size, width * size), bf16),
        pltpu.VMEM((2, *full), f32), pltpu.VMEM((2, *full), f32),
        pltpu.VMEM((2, 1, 128), f32), pltpu.VMEM((chips - 1, 1, 128), f32), pltpu.VMEM((1, 128), f32),
        pltpu.SemaphoreType.DMA((3,)), pltpu.SemaphoreType.DMA((1,)), pltpu.SemaphoreType.DMA((2,)),
        pltpu.SemaphoreType.DMA((2,)), pltpu.SemaphoreType.DMA((2, W_DN, 2)),
        pltpu.SemaphoreType.DMA((2, parts, 2)), pltpu.SemaphoreType.DMA((2, 2, 2)),
        pltpu.SemaphoreType.DMA((2,)), pltpu.SemaphoreType.DMA((2, chips - 1)), pltpu.SemaphoreType.DMA((2,)),
        pltpu.SemaphoreType.REGULAR((max(1, chips.bit_length()),)),
    ]
    return pl.pallas_call(
        functools.partial(kernel, n),
        out_shape=(
            jax.ShapeDtypeStruct((1, 2, *full), f32),
            jax.ShapeDtypeStruct((1, *full), f32),
        ),
        in_specs=[pl.BlockSpec(memory_space=pltpu.SMEM), hbm, hbm, hbm],
        out_specs=(hbm, pl.BlockSpec(memory_space=pltpu.VMEM)),
        scratch_shapes=scratch,
        compiler_params=pltpu.CompilerParams(
            collective_id=0, has_side_effects=True, vmem_limit_bytes=60 * 1024 * 1024
        ),
    )(sector_size, site_tensor, left_env, right_env)


def solution(mesh):
    block = P(("real", "row"), None, None, None)
    return jax.shard_map(
        functools.partial(on_device, mesh.shape["row"]),
        mesh=mesh,
        in_specs=(block, block, block, P("real")),
        out_specs=(block, P(("real", "row"), None, None)),
        check_vma=False,
    )
```

time: 74.2 us -> 67.3 us (0.907)
  Pallas kernels: 69.8 us -> 62.9 us
    pallas_call x1, Pallas kernels: 69.8 us -> 62.9 us  [on_device(): pl.pallas_call(functools.partial(kernel, n), out_shape=(jax.ShapeDtypeStr...]
where the time goes in v1:
time: 67.3 us; the launch traced here: 67.1 us
  Pallas kernels  62.9 us (93%)
  local copies, waits for them, and re-layouts  3.54 us (5%)
    pallas_call x1, Pallas kernels, on_device(): pl.pallas_call(functools.partial(kernel, n), out_shape=(jax.ShapeDtypeStr...  62.9 us
    unnamed x2, local copies, waits for them, and re-layouts  3.54 us

profile of v1, /device:TPU:37, one launch (start us, length us, event | category | flops | bytes accessed | tf_op | source)
XLA Modules:
  0.0 67.1 jit_solution(5383627743355746911)
XLA Ops:
  0.6 62.9 %shard_map.59 = (f32[1,2,256,256]{3,2,1,0:T(8,128)}, f32[1,256,256]{2,1,0:T(8,128)}) custom-call(s32[64]{0:T(128)} %sizes.1, f32[1,2,256,256]{3,2,1,0:T(8,128)} %site.1, f32[1,14,256,256]{3,2,1,0:T(8,128)} %left_env.1, f32[1,14,256,256]{3,2,1,0:T(8,128)} %right_env.1), custom_call_target="tpu_custom_call" | custom-call | tf_op jit(solution)/shard_map/pallas_call | solution.py:417
  63.6 1.9 %copy.8 = f32[1,2,256,256]{3,2,1,0:T(8,128)} copy(f32[1,2,256,256]{3,2,1,0:T(8,128)} %get-tuple-element.4) | data formatting | bytes 1048576
  65.4 1.7 %copy.9 = f32[1,256,256]{2,1,0:T(8,128)} copy(f32[1,256,256]{2,1,0:T(8,128)} %get-tuple-element.5) | data formatting | bytes 524288

commit v2 on v1

--- a/solution.py
+++ b/solution.py
@@ -323,6 +323,11 @@
         copy.wait_recv()
     stage_one(own_n, met_n, app_n[...])
     part_v[...] = stage_two(0, met_n)
+    greeted(3)
+    for i in range(4, len(rounds)):
+        greet(i)
+        greeted(i)
+    pl.semaphore_signal(known_sem.at[len(rounds)], inc=1, device_id=near, device_id_type=MESH)
     b, a = bond[...], app[...]
     pieces = [total_of(x) for x in (b * b, b * a, a * a)]
     for copy in app_sends[0::2]:
@@ -335,39 +340,39 @@
     packed = jnp.zeros((1, 128), f32)
     for i, piece in enumerate(pieces):
         packed = jnp.where(lane_1 == i, piece, packed)
-    mine[0] = packed
-    greeted(3)
-    for i in range(4, len(rounds)):
-        greet(i)
-        greeted(i)
-
-    def far(d):
+    mine[...] = packed
+    pl.semaphore_wait(known_sem.at[len(rounds)], 1)
+
+    def far(d, core):
+        slot = (chips - 1) * core + d - 1
         return pltpu.make_async_remote_copy(
-            src_ref=mine.at[0], dst_ref=slots.at[d - 1], send_sem=far_sem.at[0, d - 1], recv_sem=far_sem.at[1, d - 1],
-            device_id={"row": lax.rem(me + 2 * d, n)}, device_id_type=MESH,
+            src_ref=mine, dst_ref=slots.at[slot], send_sem=far_sem.at[0, slot], recv_sem=far_sem.at[1, slot],
+            device_id={"row": lax.rem(me + 2 * d, n) + core * (1 - 2 * odd)}, device_id_type=MESH,
         )
+
+    swap = remote(mine, partner, pair_sem, near)
 
     def send_far(i, _):
         d = chips // 2 + (i + 1) // 2 * (2 * (i % 2) - 1)
-        far(d).start()
+        far(d, 0).start()
+        far(d, 1).start()
         return 0
 
     lax.fori_loop(0, chips - 1, send_far, 0)
+    swap.start()
 
     result_v[0] = ortho_rows(0)
     store_up = pltpu.make_async_copy(result_v.at[0], left_out.at[0, 0], out_sem.at[0])
     store_up.start()
 
     def take_far(i, _):
-        far(i + 1).wait_recv()
+        far(i + 1, 0).wait_recv()
+        far(i + 1, 1).wait_recv()
         return 0
 
     lax.fori_loop(0, chips - 1, take_far, 0)
-    mine[1] = mine[0] + jnp.sum(slots[...], axis=0)
-    swap = remote(mine.at[1], partner, pair_sem, near)
-    swap.start()
     swap.wait_recv()
-    sums = mine[1] + partner[...]
+    sums = mine[...] + partner[...] + jnp.sum(slots[...], axis=0)
     bb, ba, aa, bh, ah, hh = (jnp.broadcast_to(sums[:, i : i + 1], (1, size)) for i in range(6))
     step = ba / bb
     weight_b = 1.0 - step + 0.5 * step * step
@@ -380,7 +385,8 @@
     bond_out[0] = (weight_b * bond[...] + weight_a * app[...] + second[...]) * scale
 
     def sent_far(i, _):
-        far(i + 1).wait_send()
+        far(i + 1, 0).wait_send()
+        far(i + 1, 1).wait_send()
         return 0
 
     lax.fori_loop(0, chips - 1, sent_far, 0)
@@ -407,11 +413,11 @@
         *[pltpu.VMEM(full, f32)] * 7,
         pltpu.VMEM((size, width * size), bf16), pltpu.VMEM((size, width * size), bf16),
         pltpu.VMEM((2, *full), f32), pltpu.VMEM((2, *full), f32),
-        pltpu.VMEM((2, 1, 128), f32), pltpu.VMEM((chips - 1, 1, 128), f32), pltpu.VMEM((1, 128), f32),
+        pltpu.VMEM((1, 128), f32), pltpu.VMEM((2 * chips - 2, 1, 128), f32), pltpu.VMEM((1, 128), f32),
         pltpu.SemaphoreType.DMA((3,)), pltpu.SemaphoreType.DMA((1,)), pltpu.SemaphoreType.DMA((2,)),
         pltpu.SemaphoreType.DMA((2,)), pltpu.SemaphoreType.DMA((2, W_DN, 2)),
         pltpu.SemaphoreType.DMA((2, parts, 2)), pltpu.SemaphoreType.DMA((2, 2, 2)),
-        pltpu.SemaphoreType.DMA((2,)), pltpu.SemaphoreType.DMA((2, chips - 1)), pltpu.SemaphoreType.DMA((2,)),
+        pltpu.SemaphoreType.DMA((2,)), pltpu.SemaphoreType.DMA((2, 2 * chips - 2)), pltpu.SemaphoreType.DMA((2,)),
         pltpu.SemaphoreType.REGULAR((max(1, chips.bit_length()),)),
     ]
     return pl.pallas_call(
@@ -424,7 +430,7 @@
         out_specs=(hbm, pl.BlockSpec(memory_space=pltpu.VMEM)),
         scratch_shapes=scratch,
         compiler_params=pltpu.CompilerParams(
-            collective_id=0, has_side_effects=True, vmem_limit_bytes=60 * 1024 * 1024
+            collective_id=0, has_side_effects=True, vmem_limit_bytes=53 * 1024 * 1024
         ),
     )(sector_size, site_tensor, left_env, right_env)
 

time: 67.3 us -> 65 us (0.966)
  local copies, waits for them, and re-layouts: 3.54 us -> 2.15 us
  Pallas kernels: 62.9 us -> 62.1 us
    unnamed x2 -> x4, local copies, waits for them, and re-layouts: 3.54 us -> 2.15 us
    pallas_call x1, Pallas kernels: 62.9 us -> 62.1 us  [on_device(): pl.pallas_call(functools.partial(kernel, n), out_shape=(jax.ShapeDtypeStr...]
where the time goes in v2:
time: 65 us; the launch traced here: 64.9 us
  Pallas kernels  62.1 us (96%)
  local copies, waits for them, and re-layouts  2.15 us (3%)
  between operations  0.65 us (1%)
    pallas_call x1, Pallas kernels, on_device(): pl.pallas_call(functools.partial(kernel, n), out_shape=(jax.ShapeDtypeStr...  62.1 us
    unnamed x4, local copies, waits for them, and re-layouts  2.15 us

profile of v2, /device:TPU:37, one launch (start us, length us, event | category | flops | bytes accessed | tf_op | source)
XLA Modules:
  0.0 64.9 jit_solution(5455032880369329988)
XLA Ops:
  0.6 0.0 copy-start
  0.6 0.6 copy-done
  1.3 62.1 %shard_map.59 = (f32[1,2,256,256]{3,2,1,0:T(8,128)S(1)}, f32[1,256,256]{2,1,0:T(8,128)S(1)}) custom-call(s32[64]{0:T(128)S(1)} %copy-done, f32[1,2,256,256]{3,2,1,0:T(8,128)} %site.1, f32[1,14,256,256]{3,2,1,0:T(8,128)} %left_env.1, f32[1,14,256,256]{3,2,1,0:T(8,128)} %right_env.1), custom_call_target="tpu_custom_call" | custom-call | tf_op jit(solution)/shard_map/pallas_call | solution.py:423
  63.4 0.8 %copy.8 = f32[1,2,256,256]{3,2,1,0:T(8,128)} copy(f32[1,2,256,256]{3,2,1,0:T(8,128)S(1)} %get-tuple-element.4) | data formatting | bytes 1048576
  64.2 0.7 %copy.9 = f32[1,256,256]{2,1,0:T(8,128)} copy(f32[1,256,256]{2,1,0:T(8,128)S(1)} %get-tuple-element.5) | data formatting | bytes 524288
Async XLA Ops:
  0.6 0.7 %copy-start = (s32[64]{0:T(128)S(1)}, s32[64]{0:T(128)}, u32[]{:S(2)}) copy-start(s32[64]{0:T(128)} %sizes.1) | copy-start | bytes 772

commit v3 on v2

--- a/solution.py
+++ b/solution.py
@@ -113,8 +113,8 @@
 
 
 def kernel(
-    n, sizes, site, left_env, right_env, left_out, bond_out,
-    site_v, low_v, left_f, right_f, near_f, cross_f, left_h, left_l, right_h, right_l,
+    n, size_list, site, left_env, right_env, left_out, bond_out,
+    sizes,    site_v, low_v, left_f, right_f, near_f, cross_f, left_h, left_l, right_h, right_l,
     gram, upper, bond, inv, halo_n, halo_c, app, app_n, app_c, second, part_v, mix_h, mix_l,
     ortho_v, result_v, mine, slots, partner,
     local_sem, out_sem, site_sem, near_sem, cross_sem, bond_sem, app_sem, low_sem, far_sem, pair_sem, known_sem,
@@ -141,7 +141,9 @@
     load_site = pltpu.make_async_copy(site.at[0], site_v, local_sem.at[0])
     load_left = pltpu.make_async_copy(left_env.at[0], left_f, local_sem.at[1])
     load_right = pltpu.make_async_copy(right_env.at[0, pl.ds(HALO, own_n)], right_f, local_sem.at[2])
+    load_sizes = pltpu.make_async_copy(size_list, sizes, local_sem.at[3])
     load_site.start()
+    load_sizes.start()
     load_left.start()
     load_right.start()
 
@@ -181,6 +183,7 @@
 
     greet(0)
 
+    load_sizes.wait()
     own_size = sizes[me]
     low_size = jnp.where(me == 0, 0, sizes[lax.rem(me + n - 1, n)])
 
@@ -272,22 +275,16 @@
     stage_one(own_n, met_n, bond_halo(halo_n))
     part_v[...] = stage_two(0, met_n)
 
-    def ortho_rows(part):
-        blocks = []
-        for k in range(size // BLK):
+    def ortho_columns(part, blocks):
+        for k in blocks:
             r0 = k * BLK
             c0 = r0 // 128 * 128
-            want = ortho_v[part][:, c0 : c0 + 128]
+            want = ortho_v[part, :, c0 : c0 + 128]
             if k:
-                done = jnp.concatenate(blocks, axis=1)
-                want = want - dot(done, upper[:r0, c0 : c0 + 128], precision=highest)
+                want = want - dot(result_v[part, :, :r0], upper[:r0, c0 : c0 + 128], precision=highest)
             first = r0 - c0
-            blocks.append(dot(want[:, first : first + BLK], inv[k][:, :BLK], ((1,), (1,)), precision=highest))
-        return jnp.concatenate(blocks, axis=1)
-
-    result_v[1] = ortho_rows(1)
-    move_low = remote(result_v.at[1], left_out.at[0, 1], low_sem, other(-1))
-    move_low.start()
+            want = want[:, first : first + BLK]
+            result_v[part, :, r0 : r0 + BLK] = dot(want, inv[k][:, :BLK], ((1,), (1,)), precision=highest)
 
     for copy in sends[1::2]:
         copy.wait_recv()
@@ -314,6 +311,8 @@
             copy = remote(app.at[:, at], halo.at[:, at], app_sem.at[to, side], target)
             copy.start()
             app_sends.append(copy)
+        if side == 0:
+            ortho_columns(1, range(size // BLK // 2))
 
     def total_of(x):
         return jnp.sum(jnp.sum(x, axis=0, keepdims=True), axis=1, keepdims=True)
@@ -328,6 +327,9 @@
         greet(i)
         greeted(i)
     pl.semaphore_signal(known_sem.at[len(rounds)], inc=1, device_id=near, device_id_type=MESH)
+    ortho_columns(1, range(size // BLK // 2, size // BLK))
+    move_low = remote(result_v.at[1], left_out.at[0, 1], low_sem, other(-1))
+    move_low.start()
     b, a = bond[...], app[...]
     pieces = [total_of(x) for x in (b * b, b * a, a * a)]
     for copy in app_sends[0::2]:
@@ -361,7 +363,7 @@
     lax.fori_loop(0, chips - 1, send_far, 0)
     swap.start()
 
-    result_v[0] = ortho_rows(0)
+    ortho_columns(0, range(size // BLK))
     store_up = pltpu.make_async_copy(result_v.at[0], left_out.at[0, 0], out_sem.at[0])
     store_up.start()
 
@@ -397,6 +399,30 @@
     store_up.wait()
 
 
+def store(left, bond, left_out, bond_out, sems):
+    copies = [
+        pltpu.make_async_copy(left, left_out, sems.at[0]),
+        pltpu.make_async_copy(bond, bond_out, sems.at[1]),
+    ]
+    for copy in copies:
+        copy.start()
+    for copy in copies:
+        copy.wait()
+
+
+def stored(left, bond):
+    here = pl.BlockSpec(memory_space=pltpu.VMEM)
+    out = pl.BlockSpec(memory_space=pltpu.HBM)
+    return pl.pallas_call(
+        store,
+        out_shape=(jax.ShapeDtypeStruct(left.shape, f32), jax.ShapeDtypeStruct(bond.shape, f32)),
+        in_specs=[here, here],
+        out_specs=(out, out),
+        scratch_shapes=[pltpu.SemaphoreType.DMA((2,))],
+        compiler_params=pltpu.CompilerParams(vmem_limit_bytes=4 * 1024 * 1024),
+    )(left, bond)
+
+
 def on_device(n, site_tensor, left_env, right_env, sector_size):
     size = site_tensor.shape[-1]
     width = left_env.shape[1]
@@ -405,7 +431,7 @@
     chips = n // 2
     parts = size // BLK
     scratch = [
-        pltpu.VMEM((2, *full), f32), pltpu.VMEM(full, f32), pltpu.VMEM((width, *full), f32),
+        pltpu.SMEM(sector_size.shape, jnp.int32), pltpu.VMEM((2, *full), f32), pltpu.VMEM(full, f32), pltpu.VMEM((width, *full), f32),
         pltpu.VMEM((width - HALO, *full), f32), pltpu.VMEM((W_DN, *full), f32), pltpu.VMEM((W_UP, *full), f32),
         pltpu.VMEM((width, *full), bf16), pltpu.VMEM((width, *full), bf16),
         pltpu.VMEM((width * size, size), bf16), pltpu.VMEM((width * size, size), bf16),
@@ -414,25 +440,26 @@
         pltpu.VMEM((size, width * size), bf16), pltpu.VMEM((size, width * size), bf16),
         pltpu.VMEM((2, *full), f32), pltpu.VMEM((2, *full), f32),
         pltpu.VMEM((1, 128), f32), pltpu.VMEM((2 * chips - 2, 1, 128), f32), pltpu.VMEM((1, 128), f32),
-        pltpu.SemaphoreType.DMA((3,)), pltpu.SemaphoreType.DMA((1,)), pltpu.SemaphoreType.DMA((2,)),
+        pltpu.SemaphoreType.DMA((4,)), pltpu.SemaphoreType.DMA((1,)), pltpu.SemaphoreType.DMA((2,)),
         pltpu.SemaphoreType.DMA((2,)), pltpu.SemaphoreType.DMA((2, W_DN, 2)),
         pltpu.SemaphoreType.DMA((2, parts, 2)), pltpu.SemaphoreType.DMA((2, 2, 2)),
         pltpu.SemaphoreType.DMA((2,)), pltpu.SemaphoreType.DMA((2, 2 * chips - 2)), pltpu.SemaphoreType.DMA((2,)),
         pltpu.SemaphoreType.REGULAR((max(1, chips.bit_length()),)),
     ]
-    return pl.pallas_call(
+    left, bond = pl.pallas_call(
         functools.partial(kernel, n),
         out_shape=(
             jax.ShapeDtypeStruct((1, 2, *full), f32),
             jax.ShapeDtypeStruct((1, *full), f32),
         ),
-        in_specs=[pl.BlockSpec(memory_space=pltpu.SMEM), hbm, hbm, hbm],
+        in_specs=[hbm, hbm, hbm, hbm],
         out_specs=(hbm, pl.BlockSpec(memory_space=pltpu.VMEM)),
         scratch_shapes=scratch,
         compiler_params=pltpu.CompilerParams(
             collective_id=0, has_side_effects=True, vmem_limit_bytes=53 * 1024 * 1024
         ),
-    )(sector_size, site_tensor, left_env, right_env)
+    )(pltpu.with_memory_space_constraint(sector_size, pltpu.HBM), site_tensor, left_env, right_env)
+    return stored(left, bond)
 
 
 def solution(mesh):

time: 65 us -> 65.4 us (level)
  Pallas kernels: 62.1 us -> 64.5 us
  local copies, waits for them, and re-layouts: 2.15 us -> 0 us
    unnamed x4 -> x0, local copies, waits for them, and re-layouts: 2.15 us -> none
    pallas_call x1, Pallas kernels: 62.1 us -> 63.6 us  [on_device(): pl.pallas_call(functools.partial(kernel, n), out_shape=(jax.ShapeDtypeStr...]
    pallas_call x0 -> x1, Pallas kernels: none -> 0.89 us  [stored(): pl.pallas_call(store, out_shape=(jax.ShapeDtypeStruct(left.shape, f32), j...]
where the time goes in v3:
time: 65.4 us; the launch traced here: 65.3 us
  Pallas kernels  64.5 us (99%)
  between operations  0.8 us (1%)
    pallas_call x1, Pallas kernels, on_device(): pl.pallas_call(functools.partial(kernel, n), out_shape=(jax.ShapeDtypeStr...  63.6 us

profile of v3, /device:TPU:37, one launch (start us, length us, event | category | flops | bytes accessed | tf_op | source)
XLA Modules:
  0.0 65.3 jit_solution(9974493171535507401)
XLA Ops:
  0.6 63.6 %shard_map.59 = (f32[1,2,256,256]{3,2,1,0:T(8,128)S(1)}, f32[1,256,256]{2,1,0:T(8,128)S(1)}) custom-call(s32[64]{0:T(128)} %size_list.1, f32[1,2,256,256]{3,2,1,0:T(8,128)} %site.1, f32[1,14,256,256]{3,2,1,0:T(8,128)} %left_env.1, f32[1,14,256,256]{3,2,1,0:T(8,128)} %right_env.1), custom_call_target="tpu_custom_call" | custom-call | tf_op jit(solution)/shard_map/pallas_call | solution.py:449
  64.2 0.9 %shard_map.60 = (f32[1,2,256,256]{3,2,1,0:T(8,128)}, f32[1,256,256]{2,1,0:T(8,128)}) custom-call(f32[1,2,256,256]{3,2,1,0:T(8,128)S(1)} %get-tuple-element.4.left, f32[1,256,256]{2,1,0:T(8,128)S(1)} %get-tuple-element.5.bond), custom_call_target="tpu_custom_call" | custom-call | tf_op jit(solution)/shard_map/pallas_call | solution.py:416

commit v4 on v3

--- a/solution.py
+++ b/solution.py
@@ -311,8 +311,6 @@
             copy = remote(app.at[:, at], halo.at[:, at], app_sem.at[to, side], target)
             copy.start()
             app_sends.append(copy)
-        if side == 0:
-            ortho_columns(1, range(size // BLK // 2))
 
     def total_of(x):
         return jnp.sum(jnp.sum(x, axis=0, keepdims=True), axis=1, keepdims=True)
@@ -327,9 +325,6 @@
         greet(i)
         greeted(i)
     pl.semaphore_signal(known_sem.at[len(rounds)], inc=1, device_id=near, device_id_type=MESH)
-    ortho_columns(1, range(size // BLK // 2, size // BLK))
-    move_low = remote(result_v.at[1], left_out.at[0, 1], low_sem, other(-1))
-    move_low.start()
     b, a = bond[...], app[...]
     pieces = [total_of(x) for x in (b * b, b * a, a * a)]
     for copy in app_sends[0::2]:
@@ -363,6 +358,9 @@
     lax.fori_loop(0, chips - 1, send_far, 0)
     swap.start()
 
+    ortho_columns(1, range(size // BLK))
+    move_low = remote(result_v.at[1], left_out.at[0, 1], low_sem, other(-1))
+    move_low.start()
     ortho_columns(0, range(size // BLK))
     store_up = pltpu.make_async_copy(result_v.at[0], left_out.at[0, 0], out_sem.at[0])
     store_up.start()

time: 65.4 us -> 63.3 us (0.968)
  Pallas kernels: 64.5 us -> 62.4 us
    pallas_call x1, Pallas kernels: 63.6 us -> 61.5 us  [on_device(): pl.pallas_call(functools.partial(kernel, n), out_shape=(jax.ShapeDtypeStr...]
where the time goes in v4:
time: 63.3 us; the launch traced here: 63.2 us
  Pallas kernels  62.4 us (99%)
  between operations  0.8 us (1%)
    pallas_call x1, Pallas kernels, on_device(): pl.pallas_call(functools.partial(kernel, n), out_shape=(jax.ShapeDtypeStr...  61.5 us

profile of v4, /device:TPU:37, one launch (start us, length us, event | category | flops | bytes accessed | tf_op | source)
XLA Modules:
  0.0 63.2 jit_solution(1796554133537253094)
XLA Ops:
  0.6 61.5 %shard_map.59 = (f32[1,2,256,256]{3,2,1,0:T(8,128)S(1)}, f32[1,256,256]{2,1,0:T(8,128)S(1)}) custom-call(s32[64]{0:T(128)} %size_list.1, f32[1,2,256,256]{3,2,1,0:T(8,128)} %site.1, f32[1,14,256,256]{3,2,1,0:T(8,128)} %left_env.1, f32[1,14,256,256]{3,2,1,0:T(8,128)} %right_env.1), custom_call_target="tpu_custom_call" | custom-call | tf_op jit(solution)/shard_map/pallas_call | solution.py:447
  62.1 0.9 %shard_map.60 = (f32[1,2,256,256]{3,2,1,0:T(8,128)}, f32[1,256,256]{2,1,0:T(8,128)}) custom-call(f32[1,2,256,256]{3,2,1,0:T(8,128)S(1)} %get-tuple-element.4.left, f32[1,256,256]{2,1,0:T(8,128)S(1)} %get-tuple-element.5.bond), custom_call_target="tpu_custom_call" | custom-call | tf_op jit(solution)/shard_map/pallas_call | solution.py:414
